TPU v7x, 256 devices: a whole 4x4x8 slice. The times are simulated.
256 devices in a mesh: row: 32 (over z, x), col: 8 (over y, core).
Axes of the slice: x: 4, y: 4, z: 8, core: 2. Of those that a mesh axis runs over, the one named last changes fastest.
Arguments:
- integrals: bfloat16 [65536, 8192], P('row', 'col'), may hold values from -0.0234375 to 0.0234375
- lambda2: bfloat16 [2016, 65536], P('col', 'row'), may hold values from -6 to 6
- source_terms: float32 [2016, 8192], P('row', 'col'), may hold values from -6 to 6
- hist_amp: bfloat16 [5, 2016, 8192], P(None, 'row', 'col'), may hold values from -6 to 6
- hist_err: bfloat16 [5, 2016, 8192], P(None, 'row', 'col'), may hold values from -64 to 64
- eps_occ: float32 [64], replicated, may hold values from -1 to -0.3
- eps_vir: float32 [800], replicated, may hold values from 0.1 to 1
- occ_pair: int32 [2, 2016], P(None, 'row'), may hold values from 0 to 63, as said below
- vir_pair: int32 [2, 8192], P(None, 'col'), may hold values from 0 to 799, as said below
Outputs:
- updated: float32 [2016, 8192], P('row', 'col')
Inputs may be any that keep to these rules, and one draw needn't show every extreme that they name: `occ_pair`: every pair i < j of the 64 occupied orbitals appears exactly once, in some order. `vir_pair`: in every column the first orbital is smaller than the second.
All inputs are finite; a program needn't handle non-finite values.
Results may differ from a plain program's by a relative error of at most 0.0003.
Values may be sent and summed in bfloat16 or wider, within the bound.
A program may use at most 64 MiB of HBM per device.

v0:
```python
import jax
import jax.numpy as jnp
from jax import lax
from jax.sharding import PartitionSpec as P

precise = lax.Precision.HIGHEST


def pair_energy(pairs, energies):
    levels = jnp.arange(energies.shape[0], dtype=jnp.int32)
    first = jnp.sum(jnp.where(pairs[0][:, None] == levels[None, :], energies[None, :], 0.0), axis=1)
    second = jnp.sum(
        jnp.where(pairs[1][:, None] == levels[None, :], energies[None, :], 0.0), axis=1
    )
    return first + second


def diis_weights(correlation):
    factor = jnp.linalg.cholesky(correlation)
    order = correlation.shape[0]
    forward = []
    for k in range(order):
        running = jnp.ones((), correlation.dtype)
        for m in range(k):
            running = running - factor[k, m] * forward[m]
        forward.append(running / factor[k, k])
    backward = [None] * order
    for k in reversed(range(order)):
        running = forward[k]
        for m in range(k + 1, order):
            running = running - factor[m, k] * backward[m]
        backward[k] = running / factor[k, k]
    solved = jnp.stack(backward)
    return solved / jnp.sum(solved)


def on_device(
    integrals, lambda2, source_terms, hist_amp, hist_err, eps_occ, eps_vir, occ_pair, vir_pair
):
    stored_count = hist_err.shape[0]
    flat_stored = hist_err.astype(jnp.float32).reshape(stored_count, -1)
    all_cols = lax.all_gather(lambda2, "col", axis=0, tiled=True)
    ladder = lax.psum_scatter(
        jnp.dot(all_cols, integrals, preferred_element_type=jnp.float32),
        "row",
        scatter_dimension=0,
        tiled=True,
    )
    denominator = pair_energy(occ_pair, eps_occ)[:, None] - pair_energy(vir_pair, eps_vir)[None, :]
    raw_update = (source_terms + ladder) / denominator
    err_new = raw_update - hist_amp[0].astype(jnp.float32)
    flat_new = err_new.reshape(1, -1)
    stacked = jnp.concatenate([flat_stored, flat_new], axis=0)
    correlation = lax.psum(jnp.dot(stacked, stacked.T, precision=precise), ("row", "col"))
    weights = diis_weights(correlation)
    updated = weights[stored_count] * raw_update
    for k in range(stored_count):
        updated = updated + weights[k] * hist_amp[k].astype(jnp.float32)
    return updated


def solution(mesh):
    placed = (
        P("row", "col"),
        P("col", "row"),
        P("row", "col"),
        P(None, "row", "col"),
        P(None, "row", "col"),
        P(),
        P(),
        P(None, "row"),
        P(None, "col"),
    )
    return jax.shard_map(
        on_device, mesh=mesh, in_specs=placed, out_specs=P("row", "col"), check_vma=False
    )
```

profile of v0, /device:TPU:1, one launch (start us, length us, event | category | flops | bytes accessed | tf_op | source)
XLA Modules:
  0.0 320.9 jit_solution(15406420744793112163)
XLA Ops:
  6.5 0.7 all-gather.3.cloned.1.call-update
  7.3 0.8 fusion.14
  8.0 1.5 select_reduce_fusion
  9.6 1.2 convert_bitcast_fusion
  10.8 54.8 %all-gather.3.cloned.1.call-done = bf16[8,252,2048]{2,1,0:T(8,128)(2,1)} async-done(((bf16[1,252,2048]{2,1,0:T(8,128)(2,1)}), bf16[8,252,2048]{2,1,0:T(8,128)(2,1)}) %all-gather.3.cloned.1.call-update) | async-done | bytes 8257552 | tf_op jit(solution)/shard_map/all_gather | solution.py:42
  65.7 7.5 %reshape.68 = bf16[2016,2048]{1,0:T(8,128)(2,1)} reshape(bf16[8,252,2048]{2,1,0:T(8,128)(2,1)} %all-gather.3.cloned.1.call-done) | data formatting | bytes 16515072
  73.1 14.2 %fusion.18 = f32[2016,1024]{1,0:T(8,128)} fusion(bf16[2016,2048]{1,0:T(8,128)(2,1)} %reshape.68, bf16[2048,1024]{1,0:T(8,128)(2,1)} %param.9), kind=kOutput, calls=%fused_computation.38 | convolution fusion | flops 8455716864 | bytes 20709376 | tf_op jit(solution)/shard_map/dot_general | solution.py:44
  87.4 100.2 %fusion = f32[64,1024]{1,0:T(8,128)S(1)} fusion(f32[2016,1024]{1,0:T(8,128)} %fusion.18), kind=kCustom, calls=%all-reduce-scatter | all-reduce-scatter fusion | flops 2097153 | bytes 8520704
  187.6 2.3 collective-permute-start
  190.0 0.8 copy.19
  190.8 0.6 dynamic-slice.4
  192.0 0.2 select_reduce_fusion.2
  192.2 2.0 concatenate.4
  194.2 1.1 fusion.5
  195.3 0.3 copy.20
  195.6 4.5 %fusion.1 = f32[6,6]{0,1:T(8,128)S(1)} fusion(f32[1,64512]{1,0:T(1,128)S(1)} %bitcast.70, f32[5,64512]{1,0:T(8,128)S(1)} %bitcast.68), kind=kOutput, calls=%fused_computation.4 | convolution fusion | flops 28256256 | bytes 1548432 | tf_op jit(solution)/shard_map/dot_general | solution.py:54
  200.1 78.7 %psum.7 = f32[6,6]{0,1:T(8,128)S(1)} all-reduce(f32[6,6]{0,1:T(8,128)S(1)} %fusion.1), channel_id=1, replica_groups=mesh['row'=32,'col'=8] {'row','col'}, use_global_device_ids=true, to_apply=%region_5.6 | all-reduce | flops 36 | bytes 288 | tf_op jit(solution)/shard_map/psum | solution.py:54
  278.9 0.5 cholesky.18
  279.4 0.6 compare_reduce_fusion
  280.1 0.6 select_select_fusion
  280.7 0.6 fusion.16
  281.3 0.7 fusion.15
  308.7 0.7 fusion.17
  309.4 4.6 %fusion.10 = f32[63,1024]{1,0:T(8,128)} fusion(bf16[5,63,1024]{2,1,0:T(8,128)(2,1)S(1)} %copy-done.2, f32[]{:T(128)} %bitcast.43, f32[]{:T(128)} %bitcast.41, f32[]{:T(128)} %bitcast.39, f32[]{:T(128)} %bitcast.37, f32[]{:T(128)} %bitcast.35, f32[]{:T(128)} %bitcast.34, f32[1024]{0:T(1024)S(1)} %add.47, f32[63]{0:T(128)S(1)} %add.46, ...), kind=kLoop, calls=%fused_computation.16 | loop fusion | flops 1225728 | bytes 1423640 | tf_op jit(solution)/shard_map/add | solution.py:58
  (23 shorter events, 0.3 us)
Async XLA Ops:
  6.5 59.1 %all-gather.3.cloned.1.call-start = ((), (), s32[]{:S(2)}) async-start(), calls=%async_computation | async-start | bytes 9437184 | tf_op jit(solution)/shard_map/all_gather | solution.py:42
  87.4 102.6 %copy-start.3 = (s32[2,63]{1,0:T(2,128)S(1)}, s32[2,63]{1,0:T(2,128)}, u32[]{:S(2)}) copy-start(s32[2,63]{1,0:T(2,128)} %param.16) | copy-start | bytes 1516
  187.6 2.4 copy-start
  187.6 3.2 copy-start.5
  187.6 4.3 %copy-start.4 = (f32[64]{0:T(128)S(1)}, f32[64]{0:T(128)}, u32[]{:S(2)}) copy-start(f32[64]{0:T(128)} %param.14) | copy-start | bytes 772
  187.6 4.5 %collective-permute-start = (f32[31,1024]{1,0:T(8,128)S(1)}, f32[31,1024]{1,0:T(8,128)}, u32[]{:S(2)}, u32[]{:S(2)}) collective-permute-start(f32[31,1024]{1,0:T(8,128)S(1)} %slice.172), channel_id=1, source_target_pairs={{0,8},{8,16},{16,24},{24,32},{32,40},{40,48},{48,56},{56,64},{64,7... | collective-permute-start | bytes 380936
  190.8 118.6 %copy-start.1 = (f32[63,1024]{1,0:T(8,128)S(1)}, f32[63,1024]{1,0:T(8,128)}, u32[]{:S(2)}) copy-start(f32[63,1024]{1,0:T(8,128)} %param.11) | copy-start | bytes 774148
  190.8 118.6 %copy-start.2 = (bf16[5,63,1024]{2,1,0:T(8,128)(2,1)S(1)}, bf16[5,63,1024]{2,1,0:T(8,128)(2,1)}, u32[]{:S(2)}) copy-start(bf16[5,63,1024]{2,1,0:T(8,128)(2,1)} %param.12) | copy-start | bytes 1935364
Sparse Core Ops, SparseCore 0:
  9.2 56.4 all-gather.2
where the time goes:
time: 322 us; the launch traced here: 321 us
  blocking collectives  179 us (56%)
  waiting for transfers between devices  55.6 us (17%)
  between operations  40.7 us (13%)
  matrix products  18.7 us (6%)
  local copies, waits for them, and re-layouts  14.1 us (4%)
  other arithmetic  10.6 us (3%)
    unnamed x1, blocking collectives  100 us
    psum x1, blocking collectives, on_device(): lax.psum(jnp.dot(stacked, stacked.T, precision=precise), ('row', 'col'))  78.7 us
    all_gather x1, waiting for transfers between devices, on_device(): all_cols = lax.all_gather(lambda2, 'col', axis=0, tiled=True)  54.8 us
    dot_general x1, matrix products, on_device(): jnp.dot(all_cols, integrals, preferred_element_type=jnp.float32)  14.2 us
    unnamed x18, local copies, waits for them, and re-layouts  11.2 us
  transfers between devices with their start and end apart: 2, of which 1 were waited for; matrix products, arithmetic and copies ran while one was open for 2% of the time, Pallas kernels for 0%

commit v1 on v0

--- a/solution.py
+++ b/solution.py
@@ -51,7 +51,9 @@
     err_new = raw_update - hist_amp[0].astype(jnp.float32)
     flat_new = err_new.reshape(1, -1)
     stacked = jnp.concatenate([flat_stored, flat_new], axis=0)
-    correlation = lax.psum(jnp.dot(stacked, stacked.T, precision=precise), ("row", "col"))
+    correlation = jnp.sum(
+        lax.all_gather(jnp.dot(stacked, stacked.T, precision=precise), ("row", "col")), axis=0
+    )
     weights = diis_weights(correlation)
     updated = weights[stored_count] * raw_update
     for k in range(stored_count):

time: 322 us -> 310 us (0.963)
  blocking collectives: 179 us -> 167 us
    psum x1 -> x0, blocking collectives: 78.7 us -> none  [on_device(): lax.psum(jnp.dot(stacked, stacked.T, precision=precise), ('row', 'col'))]
    all_gather x0 -> x1, blocking collectives: none -> 66.5 us  [on_device(): lax.all_gather(jnp.dot(stacked, stacked.T, precision=precise), ('row', 'c...]
where the time goes in v1:
time: 310 us; the launch traced here: 309 us
  blocking collectives  167 us (54%)
  waiting for transfers between devices  55.6 us (18%)
  between operations  40.7 us (13%)
  matrix products  18.9 us (6%)
  local copies, waits for them, and re-layouts  14.1 us (5%)
  other arithmetic  11 us (4%)
    unnamed x1, blocking collectives  100 us
    all_gather x1, blocking collectives, on_device(): lax.all_gather(jnp.dot(stacked, stacked.T, precision=precise), ('row', 'c...  66.5 us
    all_gather x1, waiting for transfers between devices, on_device(): all_cols = lax.all_gather(lambda2, 'col', axis=0, tiled=True)  54.8 us
    dot_general x1, matrix products, on_device(): jnp.dot(all_cols, integrals, preferred_element_type=jnp.float32)  14.2 us
    unnamed x18, local copies, waits for them, and re-layouts  11.2 us
  transfers between devices with their start and end apart: 2, of which 1 were waited for; matrix products, arithmetic and copies ran while one was open for 2% of the time, Pallas kernels for 0%

profile of v1, /device:TPU:1, one launch (start us, length us, event | category | flops | bytes accessed | tf_op | source)
XLA Modules:
  0.0 309.3 jit_solution(8957906457682440149)
XLA Ops:
  6.5 0.7 all-gather.5.cloned.1.call-update
  7.3 0.8 fusion.17
  8.0 1.5 select_reduce_fusion
  9.6 1.2 convert_bitcast_fusion
  10.8 54.8 %all-gather.5.cloned.1.call-done = bf16[8,252,2048]{2,1,0:T(8,128)(2,1)} async-done(((bf16[1,252,2048]{2,1,0:T(8,128)(2,1)}), bf16[8,252,2048]{2,1,0:T(8,128)(2,1)}) %all-gather.5.cloned.1.call-update) | async-done | bytes 8257552 | tf_op jit(solution)/shard_map/all_gather | solution.py:42
  65.7 7.5 %reshape.69 = bf16[2016,2048]{1,0:T(8,128)(2,1)} reshape(bf16[8,252,2048]{2,1,0:T(8,128)(2,1)} %all-gather.5.cloned.1.call-done) | data formatting | bytes 16515072
  73.1 14.2 %fusion.21 = f32[2016,1024]{1,0:T(8,128)} fusion(bf16[2016,2048]{1,0:T(8,128)(2,1)} %reshape.69, bf16[2048,1024]{1,0:T(8,128)(2,1)} %param.9), kind=kOutput, calls=%fused_computation.39 | convolution fusion | flops 8455716864 | bytes 20709376 | tf_op jit(solution)/shard_map/dot_general | solution.py:44
  87.4 100.2 %fusion = f32[64,1024]{1,0:T(8,128)S(1)} fusion(f32[2016,1024]{1,0:T(8,128)} %fusion.21), kind=kCustom, calls=%all-reduce-scatter | all-reduce-scatter fusion | flops 2097153 | bytes 8520704
  187.6 2.3 collective-permute-start
  190.0 0.8 copy.14
  190.8 0.6 dynamic-slice.4
  192.2 2.0 concatenate.4
  194.2 1.2 fusion.8
  195.4 0.3 copy.15
  195.7 4.7 %fusion.5 = f32[1,6,6]{2,1,0:T(8,128)S(1)} fusion(f32[1,64512]{1,0:T(1,128)S(1)} %bitcast.72, f32[5,64512]{1,0:T(8,128)S(1)} %bitcast.70), kind=kOutput, calls=%fused_computation.9 | convolution fusion | flops 28256256 | bytes 1548432 | tf_op jit(solution)/shard_map/dot_general | solution.py:55
  200.3 66.5 %all-gather.2 = f32[256,6,6]{2,1,0:T(8,128)S(1)} all-gather(f32[1,6,6]{2,1,0:T(8,128)S(1)} %fusion.5), channel_id=2, replica_groups=mesh['row'=32,'col'=8] {'row','col'}, dimensions={0}, use_global_device_ids=true | all-gather | bytes 37008 | tf_op jit(solution)/shard_map/all_gather | solution.py:55
  266.8 0.3 reduce_sum.68
  267.2 0.5 cholesky.18
  267.8 0.6 compare_reduce_fusion
  268.4 0.6 select_select_fusion
  269.1 0.6 fusion.19
  269.7 0.7 fusion.18
  297.1 0.7 fusion.20
  297.8 4.6 %fusion.13 = f32[63,1024]{1,0:T(8,128)} fusion(bf16[5,63,1024]{2,1,0:T(8,128)(2,1)S(1)} %copy-done.2, f32[]{:T(128)} %bitcast.44, f32[]{:T(128)} %bitcast.42, f32[]{:T(128)} %bitcast.40, f32[]{:T(128)} %bitcast.38, f32[]{:T(128)} %bitcast.36, f32[]{:T(128)} %bitcast.35, f32[1024]{0:T(1024)S(1)} %add.45, f32[63]{0:T(128)S(1)} %add.44, ...), kind=kLoop, calls=%fused_computation.17 | loop fusion | flops 1225728 | bytes 1423640 | tf_op jit(solution)/shard_map/add | solution.py:60
  (24 shorter events, 0.5 us)
Async XLA Ops:
  6.5 59.1 %all-gather.5.cloned.1.call-start = ((), (), s32[]{:S(2)}) async-start(), calls=%async_computation | async-start | bytes 9437184 | tf_op jit(solution)/shard_map/all_gather | solution.py:42
  87.4 102.6 %copy-start.3 = (s32[2,63]{1,0:T(2,128)S(1)}, s32[2,63]{1,0:T(2,128)}, u32[]{:S(2)}) copy-start(s32[2,63]{1,0:T(2,128)} %param.16) | copy-start | bytes 1516
  187.6 2.4 copy-start
  187.6 3.2 %copy-start.5 = (u32[256]{0:T(256)S(1)}, u32[256]{0:T(256)}, u32[]{:S(2)}) copy-start(u32[256]{0:T(256)} %constant.47) | copy-start | bytes 3076
  187.6 4.3 %copy-start.4 = (f32[64]{0:T(128)S(1)}, f32[64]{0:T(128)}, u32[]{:S(2)}) copy-start(f32[64]{0:T(128)} %param.14) | copy-start | bytes 772
  187.6 4.5 %collective-permute-start = (f32[31,1024]{1,0:T(8,128)S(1)}, f32[31,1024]{1,0:T(8,128)}, u32[]{:S(2)}, u32[]{:S(2)}) collective-permute-start(f32[31,1024]{1,0:T(8,128)S(1)} %slice.172), channel_id=1, source_target_pairs={{0,8},{8,16},{16,24},{24,32},{32,40},{40,48},{48,56},{56,64},{64,7... | collective-permute-start | bytes 380936
  194.2 103.6 %copy-start.1 = (f32[63,1024]{1,0:T(8,128)S(1)}, f32[63,1024]{1,0:T(8,128)}, u32[]{:S(2)}) copy-start(f32[63,1024]{1,0:T(8,128)} %param.11) | copy-start | bytes 774148
  194.2 103.6 %copy-start.2 = (bf16[5,63,1024]{2,1,0:T(8,128)(2,1)S(1)}, bf16[5,63,1024]{2,1,0:T(8,128)(2,1)}, u32[]{:S(2)}) copy-start(bf16[5,63,1024]{2,1,0:T(8,128)(2,1)} %param.12) | copy-start | bytes 1935364
Sparse Core Ops, SparseCore 0:
  9.2 56.4 all-gather.4
